TPU v7x, 512 devices: a whole 4x8x8 slice. The times are simulated.
512 devices in a mesh: section: 4 (over y_hi), dp: 128 (over z, x, y_lo, core).
Axes of the slice: x: 4, y: 8 (y_hi: 4, y_lo: 2; y = y_hi * 2 + y_lo), z: 8, core: 2. Of those that a mesh axis runs over, the one named last changes fastest.
Arguments:
- saved_inputs: bfloat16 [4, 2, 16384, 320], P('section', None, 'dp'), may hold values from -6 to 6
- timesteps: int32 [2, 16384], P(None, 'dp'), may hold values from 0 to 999
- time_table: bfloat16 [1000, 320], replicated, may hold values from -6 to 6
- skip_weight: bfloat16 [4, 320, 320], P('section'), may hold values from -0.3125 to 0.3125
- ff_in: bfloat16 [4, 1280, 320], P('section'), may hold values from -0.3125 to 0.3125
- ff_out: bfloat16 [4, 1280, 320], P('section'), may hold values from -0.15625 to 0.15625
- output_cotangent: bfloat16 [2, 16384, 320], P(None, 'dp'), may hold values from -6 to 6
Outputs:
- input_grads: bfloat16 [4, 2, 16384, 320], P('section', None, 'dp')
- skip_weight_grad: float32 [4, 102400], P('section', 'dp')
- ff_in_grad: float32 [4, 1280, 320], P('section', 'dp')
- ff_out_grad: float32 [4, 1280, 320], P('section', 'dp')
All inputs are finite; a program needn't handle non-finite values.
Results may differ from a plain program's by a relative error of at most 0.01.
Values may be sent and summed in bfloat16 or wider, within the bound.
A program may use at most 128 MiB of HBM per device.

v0:
```python
import jax
import jax.numpy as jnp
from jax import lax
from jax.sharding import Mesh
from jax.sharding import PartitionSpec as P

DP = ("dp_0", "dp_1", "dp_2", "dp_3")


EPS = 1e-06


def from_partner(shard, axis, stride):
    return lax.ppermute(shard, axis, [(i, i ^ 1 << stride) for i in range(lax.axis_size(axis))])


def passed_along(value, axis, steps):
    count = lax.axis_size(axis)
    first, last = (max(0, -steps), min(count, count - steps))
    return lax.ppermute(value, axis, [(source, source + steps) for source in range(first, last)])


def cut_along(shard, dim, length):
    before, after = (shard.shape[:dim], shard.shape[dim + 1 :])
    return jnp.moveaxis(shard.reshape(*before, length, -1, *after), dim, 0)


def sum_at_owner(shard, axis, dim):
    length = lax.axis_size(axis)
    blocks = lax.all_to_all(cut_along(shard, dim, length), axis, 0, 0, tiled=True)
    return jnp.sum(blocks.astype(jnp.float32), axis=0)


def sum_by_axis(shard, axes, dim):
    far, near = axes
    own = sum_at_owner(cut_along(shard, dim, lax.axis_size(far)), near, dim + 1)
    return jnp.sum(
        lax.all_to_all(own.astype(jnp.bfloat16), far, 0, 0, tiled=True).astype(jnp.float32), axis=0
    )


def sent_together(arrays, axis, dim, along):
    ends, at = ([], 0)
    for a in arrays[:-1]:
        at += a.shape[along]
        ends.append(at)
    both = jnp.concatenate(arrays, axis=along)
    return tuple(jnp.split(sum_by_axis(both, axis, dim), ends, axis=along))


def contract(left, right, dims):
    return lax.dot_general(
        left, right, ((dims[0], dims[1]), ((), ())), preferred_element_type=jnp.float32
    )


def forward(inputs, source, w_skip, w_in, w_out):
    united = inputs.astype(jnp.float32) + jnp.dot(
        source, w_skip, preferred_element_type=jnp.float32
    )
    recip = lax.rsqrt(jnp.mean(united * united, axis=-1, keepdims=True) + EPS)
    normed = (united * recip).astype(jnp.bfloat16)
    preact = contract(normed, w_in, ((1,), (1,)))
    active = jax.nn.silu(preact).astype(jnp.bfloat16)
    output = united + jnp.dot(active, w_out, preferred_element_type=jnp.float32)
    return (united, recip, normed, preact, active, output)


def put_micro(buffer, value, index, valid):
    updated = lax.dynamic_update_index_in_dim(buffer, value, index, 0)
    return jnp.where(valid, updated, buffer)


def shards(saved_inputs, timesteps, time_table, skip_weight, ff_in, ff_out, output_cotangent):
    section = lax.axis_index("section")
    n_micro = saved_inputs.shape[1]
    rows = saved_inputs.shape[2]
    width = saved_inputs.shape[3]
    hidden = ff_in.shape[1]
    inputs = saved_inputs[0]
    w_skip = skip_weight[0]
    w_in = ff_in[0]
    w_out = ff_out[0]
    bit_order = (0, 1)
    levels = lax.broadcasted_iota(jnp.int32, (1, time_table.shape[0]), 1)
    embed_list = []
    value_list = []
    for micro in range(n_micro):
        onehot = (timesteps[micro][:, None] == levels).astype(jnp.bfloat16)
        embed = jnp.dot(onehot, time_table, preferred_element_type=jnp.float32).astype(jnp.bfloat16)
        embed_list.append(embed)
        value_list.append(
            forward(inputs[micro], embed, w_skip, w_in, w_out)[5].astype(jnp.bfloat16)
        )
    embeds = jnp.stack(embed_list)
    values = jnp.stack(value_list)
    received = values
    for bit in bit_order:
        received = from_partner(received, "section", bit)
    sources = jnp.where(section >= 2, received, embeds)

    def active_path(operands):
        grad_out, own_input, source = operands
        united, recip, normed, preact, active, output = forward(
            own_input, source, w_skip, w_in, w_out
        )
        grad_low = grad_out.astype(jnp.bfloat16)
        grad_act = contract(grad_low, w_out, ((1,), (1,)))
        sigma = jax.nn.sigmoid(preact)
        grad_pre = (grad_act * sigma * (1.0 + preact * (1.0 - sigma))).astype(jnp.bfloat16)
        grad_norm = jnp.dot(grad_pre, w_in, preferred_element_type=jnp.float32)
        grad_united = (
            grad_out
            + recip * grad_norm
            - united * recip**3 * jnp.mean(grad_norm * united, axis=-1, keepdims=True)
        )
        united_low = grad_united.astype(jnp.bfloat16)
        d_skip = contract(source, united_low, ((0,), (0,)))
        grad_source = contract(united_low, w_skip, ((1,), (1,))).astype(jnp.bfloat16)
        extra = (contract(grad_pre, normed, ((0,), (0,))), contract(active, grad_low, ((0,), (0,))))
        return (united_low, grad_source, d_skip) + extra

    def resting_path(operands):
        low_rows = jnp.zeros((rows, width), jnp.bfloat16)
        base = (low_rows, low_rows, jnp.zeros((width, width), jnp.float32))
        extra = (jnp.zeros((hidden, width), jnp.float32), jnp.zeros((hidden, width), jnp.float32))
        return base + extra

    chain = jnp.zeros((rows, width), jnp.bfloat16)
    skip_store = jnp.zeros((n_micro, rows, width), jnp.bfloat16)
    grad_store = jnp.zeros((n_micro, rows, width), jnp.bfloat16)
    total_skip = jnp.zeros((width, width), jnp.float32)
    total_in = jnp.zeros((hidden, width), jnp.float32)
    total_out = jnp.zeros((hidden, width), jnp.float32)
    for tick in range(n_micro + 3):
        micro = tick - (3 - section)
        valid = (micro >= 0) & (micro < n_micro)
        index = jnp.clip(micro, 0, n_micro - 1)
        own_input = lax.dynamic_index_in_dim(inputs, index, 0, keepdims=False)
        source = lax.dynamic_index_in_dim(sources, index, 0, keepdims=False)
        carried = lax.dynamic_index_in_dim(skip_store, index, 0, keepdims=False).astype(jnp.float32)
        upstream = chain.astype(jnp.float32) + jnp.where(section < 2, carried, 0.0)
        top = lax.dynamic_index_in_dim(output_cotangent, index, 0, keepdims=False).astype(
            jnp.float32
        )
        grad_out = jnp.where(section == 3, top, upstream)
        parts = lax.cond(valid, active_path, resting_path, (grad_out, own_input, source))
        united_low = parts[0]
        grad_store = put_micro(grad_store, united_low, index, valid)
        total_skip = total_skip + parts[2]
        total_in = total_in + parts[3]
        total_out = total_out + parts[4]
        chain = passed_along(united_low, "section", -1)
        back = parts[1]
        for bit in bit_order:
            back = from_partner(back, "section", bit)
        sender = tick - section
        receive = (section < 2) & (sender >= 0) & (sender < n_micro)
        skip_store = put_micro(skip_store, back, jnp.clip(sender, 0, n_micro - 1), receive)
    grad_in, grad_out_w, grad_skip = (
        *sent_together(
            (total_in.astype(jnp.bfloat16), total_out.astype(jnp.bfloat16)),
            (("dp_0", "dp_1", "dp_2"), "dp_3"),
            0,
            1,
        ),
        sum_by_axis(
            total_skip.reshape(-1).astype(jnp.bfloat16), (("dp_0", "dp_1", "dp_2"), "dp_3"), 0
        ),
    )
    return (grad_store[None], grad_skip[None], grad_in[None], grad_out_w[None])


def solution(mesh):
    split = Mesh(
        mesh.devices.reshape(mesh.shape["section"], 8, 4, 2, 2),
        ("section", "dp_0", "dp_1", "dp_2", "dp_3"),
    )
    return jax.shard_map(
        shards,
        mesh=split,
        in_specs=(
            P("section", None, DP, None),
            P(None, DP),
            P(),
            P("section", None, None),
            P("section", None, None),
            P("section", None, None),
            P(None, DP, None),
        ),
        out_specs=(
            P("section", None, DP, None),
            P("section", DP),
            P("section", DP, None),
            P("section", DP, None),
        ),
        check_vma=False,
    )
```

profile of v0, /device:TPU:1, one launch (start us, length us, event | category | flops | bytes accessed | tf_op | source)
XLA Modules:
  0.0 271.2 jit_solution(11763966970212372962)
XLA Ops:
  5.9 5.0 %collective-permute-start = (bf16[2,128,320]{1,2,0:T(8,128)(2,1)S(1)}, bf16[2,128,320]{1,2,0:T(8,128)(2,1)S(1)}, u32[]{:S(2)}, u32[]{:S(2)}) collective-permute-start(bf16[2,128,320]{1,2,0:T(8,128)(2,1)S(1)} %pad_maximum_fusion.1), channel_id=1, source_target_pairs={{0,128},{128,0},{256,384},{384,256},{1,129},{129,1},{257,385},{385... | collective-permute-start | bytes 491528 | tf_op jit(solution)/shard_map/ppermute | solution.py:14
  10.9 6.2 %collective-permute-done = bf16[2,128,320]{1,2,0:T(8,128)(2,1)S(1)} collective-permute-done((bf16[2,128,320]{1,2,0:T(8,128)(2,1)S(1)}, bf16[2,128,320]{1,2,0:T(8,128)(2,1)S(1)}, u32[]{:S(2)}, u32[]{:S(2)}) %collective-permute-start) | collective-permute-done | bytes 163872 | tf_op jit(solution)/shard_map/ppermute | solution.py:14
  17.1 9.3 %collective-permute-start.1 = (bf16[2,128,320]{1,2,0:T(8,128)(2,1)S(1)}, bf16[2,128,320]{1,2,0:T(8,128)(2,1)S(1)}, u32[]{:S(2)}, u32[]{:S(2)}) collective-permute-start(bf16[2,128,320]{1,2,0:T(8,128)(2,1)S(1)} %collective-permute-done), channel_id=1, source_target_pairs={{0,256},{128,384},{256,0},{384,128},{1,257},{129,385},{257,1},{385... | collective-permute-start | bytes 491528 | tf_op jit(solution)/shard_map/ppermute | solution.py:14
  28.4 2.3 collective-permute-done.1
  32.0 3.5 %conditional.5 = (bf16[128,320]{0,1:T(8,128)(2,1)}, bf16[128,320]{0,1:T(8,128)(2,1)S(1)}, f32[320,320]{1,0:T(8,128)}, f32[1280,320]{0,1:T(8,128)S(1)}, f32[1280,...) conditional(s32[]{:T(128)} %convert_element_type.349, () %tuple.76, (bf16[2,128,320]{1,2,0:T(8,128)(2,1)}, s32[]{:T(128)}, ...), branch_computations={%region_2.3_spmd, %region_3.6_spmd} | conditional | flops 606249344 | bytes 17243340 | solution.py:147
  35.6 1.9 collective-permute-start.2
  38.8 3.0 %collective-permute-done.2 = bf16[128,320]{0,1:T(8,128)(2,1)} collective-permute-done((bf16[128,320]{0,1:T(8,128)(2,1)S(1)}, bf16[128,320]{0,1:T(8,128)(2,1)}, u32[]{:S(2)}, u32[]{:S(2)}) %collective-permute-start.2) | collective-permute-done | bytes 81952 | tf_op jit(solution)/shard_map/ppermute | solution.py:14
  41.7 11.2 %collective-permute-start.3 = (bf16[128,320]{0,1:T(8,128)(2,1)}, bf16[128,320]{0,1:T(8,128)(2,1)}, u32[]{:S(2)}, u32[]{:S(2)}) collective-permute-start(bf16[128,320]{0,1:T(8,128)(2,1)} %collective-permute-done.2), channel_id=1, source_target_pairs={{0,256},{128,384},{256,0},{384,128},{1,257},{129,385},{257,1},{385... | collective-permute-start | bytes 245768 | tf_op jit(solution)/shard_map/ppermute | solution.py:14
  53.0 1.6 convert_element_type.363
  56.5 1.5 bitcast_dynamic-update-slice_fusion.1
  59.3 4.7 %conditional.6 = (bf16[128,320]{0,1:T(8,128)(2,1)}, bf16[128,320]{0,1:T(8,128)(2,1)S(1)}, f32[320,320]{1,0:T(8,128)}, f32[1280,320]{0,1:T(8,128)}, f32[1280,320]{0,1:T(8,128)}, /*index=5*/bf16[1,128,320]{1,2,0:T(8,128)(2,1)}) conditional(s32[]{:T(128)} %convert_element_type.362, () %tuple.78, (bf16[2,128,320]{1,2,0:T(8,128)(2,1)}, s32[]{:T(128)}, ...), branch_computations={%region_6.7_spmd, %region_7.10_spmd} | conditional | flops 606208384 | bytes 17243276 | solution.py:147
  64.0 5.4 %collective-permute-start.5 = (bf16[128,320]{0,1:T(8,128)(2,1)S(1)}, bf16[128,320]{0,1:T(8,128)(2,1)}, u32[]{:S(2)}, u32[]{:S(2)}) collective-permute-start(bf16[128,320]{0,1:T(8,128)(2,1)S(1)} %get-tuple-element.596), channel_id=1, source_target_pairs={{0,128},{128,0},{256,384},{384,256},{1,129},{129,1},{257,385},{385... | collective-permute-start | bytes 245768 | tf_op jit(solution)/shard_map/ppermute | solution.py:14
  71.4 15.3 %collective-permute-start.6 = (bf16[128,320]{0,1:T(8,128)(2,1)}, bf16[128,320]{0,1:T(8,128)(2,1)}, u32[]{:S(2)}, u32[]{:S(2)}) collective-permute-start(bf16[128,320]{0,1:T(8,128)(2,1)} %collective-permute-done.5), channel_id=1, source_target_pairs={{0,256},{128,384},{256,0},{384,128},{1,257},{129,385},{257,1},{385... | collective-permute-start | bytes 245768 | tf_op jit(solution)/shard_map/ppermute | solution.py:14
  86.7 1.6 convert_element_type.365
  88.8 1.6 fusion.120
  90.4 4.8 %conditional.7 = (bf16[128,320]{0,1:T(8,128)(2,1)}, bf16[128,320]{0,1:T(8,128)(2,1)S(1)}, f32[320,320]{1,0:T(8,128)}, f32[1280,320]{0,1:T(8,128)}, f32[1280,320]{0,1:T(8,128)}, /*index=5*/bf16[1,128,320]{1,2,0:T(8,128)(2,1)}) conditional(s32[]{:T(128)} %convert_element_type.364, () %tuple.80, (bf16[2,128,320]{1,2,0:T(8,128)(2,1)}, s32[]{:T(128)}, ...), branch_computations={%region_10.11_spmd, %region_11.14_spmd} | conditional | flops 606208384 | bytes 17243276 | solution.py:147
  95.2 15.0 %collective-permute-start.8 = (bf16[128,320]{0,1:T(8,128)(2,1)S(1)}, bf16[128,320]{0,1:T(8,128)(2,1)}, u32[]{:S(2)}, u32[]{:S(2)}) collective-permute-start(bf16[128,320]{0,1:T(8,128)(2,1)S(1)} %get-tuple-element.599), channel_id=1, source_target_pairs={{0,128},{128,0},{256,384},{384,256},{1,129},{129,1},{257,385},{385... | collective-permute-start | bytes 245768 | tf_op jit(solution)/shard_map/ppermute | solution.py:14
  112.1 7.5 %collective-permute-start.9 = (bf16[128,320]{0,1:T(8,128)(2,1)}, bf16[128,320]{0,1:T(8,128)(2,1)}, u32[]{:S(2)}, u32[]{:S(2)}) collective-permute-start(bf16[128,320]{0,1:T(8,128)(2,1)} %collective-permute-done.8), channel_id=1, source_target_pairs={{0,256},{128,384},{256,0},{384,128},{1,257},{129,385},{257,1},{385... | collective-permute-start | bytes 245768 | tf_op jit(solution)/shard_map/ppermute | solution.py:14
  119.7 1.6 convert_element_type.367
  121.9 1.6 fusion.119
  123.4 14.8 %conditional.8 = (bf16[128,320]{0,1:T(8,128)(2,1)}, bf16[128,320]{0,1:T(8,128)(2,1)S(1)}, f32[320,320]{1,0:T(8,128)}, f32[1280,320]{0,1:T(8,128)}, f32[1280,320]{0,1:T(8,128)}, /*index=5*/bf16[1,128,320]{1,2,0:T(8,128)(2,1)}) conditional(s32[]{:T(128)} %convert_element_type.366, () %tuple.82, (bf16[2,128,320]{1,2,0:T(8,128)(2,1)}, s32[]{:T(128)}, ...), branch_computations={%region_14.15_spmd, %region_15.18_spmd} | conditional | flops 606208384 | bytes 17243276 | solution.py:147
  123.4 1.7 copy.62
  129.8 1.7 convolution_convert_fusion.3
  131.5 1.9 fusion.66
  133.5 1.6 fusion.73
  135.0 1.6 fusion.62
  136.7 1.5 copy.124
  138.2 5.0 %collective-permute-start.11 = (bf16[128,320]{0,1:T(8,128)(2,1)S(1)}, bf16[128,320]{0,1:T(8,128)(2,1)}, u32[]{:S(2)}, u32[]{:S(2)}) collective-permute-start(bf16[128,320]{0,1:T(8,128)(2,1)S(1)} %get-tuple-element.602), channel_id=1, source_target_pairs={{0,128},{128,0},{256,384},{384,256},{1,129},{129,1},{257,385},{385... | collective-permute-start | bytes 245768 | tf_op jit(solution)/shard_map/ppermute | solution.py:14
  145.1 5.2 %collective-permute-start.12 = (bf16[128,320]{0,1:T(8,128)(2,1)}, bf16[128,320]{0,1:T(8,128)(2,1)}, u32[]{:S(2)}, u32[]{:S(2)}) collective-permute-start(bf16[128,320]{0,1:T(8,128)(2,1)} %collective-permute-done.11), channel_id=1, source_target_pairs={{0,256},{128,384},{256,0},{384,128},{1,257},{129,385},{257,1},{385... | collective-permute-start | bytes 245768 | tf_op jit(solution)/shard_map/ppermute | solution.py:14
  150.3 1.6 convert_element_type.369
  151.9 3.5 %collective-permute-done.12 = bf16[128,320]{0,1:T(8,128)(2,1)} collective-permute-done((bf16[128,320]{0,1:T(8,128)(2,1)}, bf16[128,320]{0,1:T(8,128)(2,1)}, u32[]{:S(2)}, u32[]{:S(2)}) %collective-permute-start.12) | collective-permute-done | bytes 81952 | tf_op jit(solution)/shard_map/ppermute | solution.py:14
  155.5 14.3 %conditional.9 = (f32[320,320]{1,0:T(8,128)S(1)}, f32[1280,320]{0,1:T(8,128)}, f32[1280,320]{0,1:T(8,128)}, bf16[1,128,320]{1,2,0:T(8,128)(2,1)}) conditional(s32[]{:T(128)} %convert_element_type.368, () %tuple.84, (bf16[2,128,320]{1,2,0:T(8,128)(2,1)}, s32[]{:T(128)}, bf16[2,128,320]{1,2,0:T(8,128)(2,1)}, s32[]{:T(128)}, pred[]{:T(512)}, ...), branch_computations={%region_18.19_spmd, %region_19.22_spmd.clone} | conditional | flops 579993984 | bytes 17284272 | solution.py:147
  155.5 1.7 copy.63
  157.2 1.9 multiply_reduce_fusion.9
  159.1 1.7 fusion.89
  166.6 1.6 fusion.92
  168.2 1.6 fusion.80
  169.8 1.6 add_convert_fusion.2
  171.9 16.0 %all_to_all.24 = bf16[2,64,800]{2,1,0:T(8,128)(2,1)S(1)} all-to-all(bf16[2,64,800]{2,1,0:T(8,128)(2,1)S(1)} %copy.64), channel_id=1, replica_groups=mesh['section'=4,'dp_0'=8,'dp_1'=4,'dp_2'=2,'dp_3'=2] {'dp_3'}, dimensions={0} | all-to-all | bytes 409600 | tf_op jit(solution)/shard_map/all_to_all | solution.py:30
  189.9 6.1 %add_convert_fusion = (bf16[1280,320]{0,1:T(8,128)(2,1)S(1)}, bf16[1280,320]{0,1:T(8,128)(2,1)S(1)}) fusion(f32[1280,320]{0,1:T(8,128)} %get-tuple-element.619, f32[1280,320]{0,1:T(8,128)} %get-tuple-element.618, f32[1280,320]{0,1:T(8,128)} %get-tuple-element.617, f32[1280,320]{0,1:T(8,128)} %get-tuple-element.615, f32[1280,320]{0,1:T(8,128)} %get-tuple-element.616, ...), kind=kLoop, calls=%fused_computation.161 | loop fusion | flops 4096000 | bytes 18022400 | tf_op jit(solution)/shard_map/convert_element_type | solution.py:162
  196.1 2.2 copy.66
  198.3 2.5 reshape_reshape.4
  201.3 5.0 %all_to_all.25 = bf16[2,64,10,640]{3,1,2,0:T(8,128)(2,1)S(1)} all-to-all(bf16[2,64,10,640]{3,1,2,0:T(8,128)(2,1)S(1)} %copy.67), channel_id=1, replica_groups=mesh['section'=4,'dp_0'=8,'dp_1'=4,'dp_2'=2,'dp_3'=2] {'dp_3'}, dimensions={0} | all-to-all | bytes 3276800 | tf_op jit(solution)/shard_map/all_to_all | solution.py:30
  206.2 16.2 %all-to-all-start.1 = ((bf16[64,2,400]{2,1,0:T(2,128)(2,1)}), bf16[64,2,400]{2,1,0:T(2,128)(2,1)S(1)}, u32[]{:S(2)}, u32[]{:S(2)}) async-start(bf16[64,2,400]{2,1,0:T(2,128)(2,1)} %reshape.197), calls=%async_computation.1 | async-start | bytes 262144 | tf_op jit(solution)/shard_map/all_to_all | solution.py:38
  223.1 1.6 copy.68
  224.7 7.4 %all-to-all-done.1 = bf16[64,2,400]{2,1,0:T(2,128)(2,1)S(1)} async-done(((bf16[64,2,400]{2,1,0:T(2,128)(2,1)}), bf16[64,2,400]{2,1,0:T(2,128)(2,1)S(1)}, u32[]{:S(2)}, u32[]{:S(2)}) %all-to-all-start.1) | async-done | bytes 102432 | tf_op jit(solution)/shard_map/all_to_all | solution.py:38
  232.1 5.4 %all-to-all-start.3 = ((bf16[64,10,640]{2,1,0:T(8,128)(2,1)}), bf16[64,10,640]{2,1,0:T(8,128)(2,1)S(1)}, u32[]{:S(2)}, u32[]{:S(2)}) async-start(bf16[64,10,640]{2,1,0:T(8,128)(2,1)} %copy.68), calls=%async_computation.3 | async-start | bytes 2621440 | tf_op jit(solution)/shard_map/all_to_all | solution.py:38
  240.6 29.1 %all-to-all-done.3 = bf16[64,10,640]{2,1,0:T(8,128)(2,1)S(1)} async-done(((bf16[64,10,640]{2,1,0:T(8,128)(2,1)}), bf16[64,10,640]{2,1,0:T(8,128)(2,1)S(1)}, u32[]{:S(2)}, u32[]{:S(2)}) %all-to-all-start.3) | async-done | bytes 819232 | tf_op jit(solution)/shard_map/all_to_all | solution.py:38
  (112 shorter events, 51.6 us)
Async XLA Ops:
  0.6 1.1 copy-start
  0.6 3.3 %copy-start.3 = (bf16[1,2,128,320]{2,3,1,0:T(8,128)(2,1)S(1)}, bf16[1,2,128,320]{2,3,1,0:T(8,128)(2,1)}, u32[]{:S(2)}) copy-start(bf16[1,2,128,320]{2,3,1,0:T(8,128)(2,1)} %param.17) | copy-start | bytes 491524
  0.7 3.3 %copy-start.1 = (bf16[1,320,320]{2,1,0:T(8,128)(2,1)S(1)}, bf16[1,320,320]{2,1,0:T(8,128)(2,1)}, u32[]{:S(2)}) copy-start(bf16[1,320,320]{2,1,0:T(8,128)(2,1)} %param.20) | copy-start | bytes 614404
  0.7 3.6 %copy-start.13 = (bf16[1,1280,320]{1,2,0:T(8,128)(2,1)S(1)}, bf16[1,1280,320]{1,2,0:T(8,128)(2,1)}, u32[]{:S(2)}) copy-start(bf16[1,1280,320]{1,2,0:T(8,128)(2,1)} %param.22) | copy-start | bytes 2457604
  0.7 3.6 %copy-start.14 = (bf16[1,1280,320]{1,2,0:T(8,128)(2,1)S(1)}, bf16[1,1280,320]{1,2,0:T(8,128)(2,1)}, u32[]{:S(2)}) copy-start(bf16[1,1280,320]{1,2,0:T(8,128)(2,1)} %param.21) | copy-start | bytes 2457604
  5.9 11.2 %collective-permute-start = (bf16[2,128,320]{1,2,0:T(8,128)(2,1)S(1)}, bf16[2,128,320]{1,2,0:T(8,128)(2,1)S(1)}, u32[]{:S(2)}, u32[]{:S(2)}) collective-permute-start(bf16[2,128,320]{1,2,0:T(8,128)(2,1)S(1)} %pad_maximum_fusion.1), channel_id=1, source_target_pairs={{0,128},{128,0},{256,384},{384,256},{1,129},{129,1},{257,385},{385... | collective-permute-start | bytes 491528 | tf_op jit(solution)/shard_map/ppermute | solution.py:14
  17.1 13.6 %collective-permute-start.1 = (bf16[2,128,320]{1,2,0:T(8,128)(2,1)S(1)}, bf16[2,128,320]{1,2,0:T(8,128)(2,1)S(1)}, u32[]{:S(2)}, u32[]{:S(2)}) collective-permute-start(bf16[2,128,320]{1,2,0:T(8,128)(2,1)S(1)} %collective-permute-done), channel_id=1, source_target_pairs={{0,256},{128,384},{256,0},{384,128},{1,257},{129,385},{257,1},{385... | collective-permute-start | bytes 491528 | tf_op jit(solution)/shard_map/ppermute | solution.py:14
  35.6 6.2 %collective-permute-start.2 = (bf16[128,320]{0,1:T(8,128)(2,1)S(1)}, bf16[128,320]{0,1:T(8,128)(2,1)}, u32[]{:S(2)}, u32[]{:S(2)}) collective-permute-start(bf16[128,320]{0,1:T(8,128)(2,1)S(1)} %get-tuple-element.593), channel_id=1, source_target_pairs={{0,128},{128,0},{256,384},{384,256},{1,129},{129,1},{257,385},{385... | collective-permute-start | bytes 245768 | tf_op jit(solution)/shard_map/ppermute | solution.py:14
  37.5 15.5 %collective-permute-start.4 = (bf16[128,320]{0,1:T(8,128)(2,1)}, bf16[128,320]{0,1:T(8,128)(2,1)}, u32[]{:S(2)}, u32[]{:S(2)}) collective-permute-start(bf16[128,320]{0,1:T(8,128)(2,1)} %get-tuple-element.594), channel_id=1, source_target_pairs={{128,0},{256,128},{384,256},{129,1},{257,129},{385,257},{130,2},{2... | collective-permute-start | bytes 245768 | tf_op jit(solution)/shard_map/ppermute | solution.py:20
  41.7 14.1 %collective-permute-start.3 = (bf16[128,320]{0,1:T(8,128)(2,1)}, bf16[128,320]{0,1:T(8,128)(2,1)}, u32[]{:S(2)}, u32[]{:S(2)}) collective-permute-start(bf16[128,320]{0,1:T(8,128)(2,1)} %collective-permute-done.2), channel_id=1, source_target_pairs={{0,256},{128,384},{256,0},{384,128},{1,257},{129,385},{257,1},{385... | collective-permute-start | bytes 245768 | tf_op jit(solution)/shard_map/ppermute | solution.py:14
  64.0 7.4 %collective-permute-start.5 = (bf16[128,320]{0,1:T(8,128)(2,1)S(1)}, bf16[128,320]{0,1:T(8,128)(2,1)}, u32[]{:S(2)}, u32[]{:S(2)}) collective-permute-start(bf16[128,320]{0,1:T(8,128)(2,1)S(1)} %get-tuple-element.596), channel_id=1, source_target_pairs={{0,128},{128,0},{256,384},{384,256},{1,129},{129,1},{257,385},{385... | collective-permute-start | bytes 245768 | tf_op jit(solution)/shard_map/ppermute | solution.py:14
  69.4 17.2 %collective-permute-start.7 = (bf16[128,320]{0,1:T(8,128)(2,1)}, bf16[128,320]{0,1:T(8,128)(2,1)}, u32[]{:S(2)}, u32[]{:S(2)}) collective-permute-start(bf16[128,320]{0,1:T(8,128)(2,1)} %get-tuple-element.597), channel_id=1, source_target_pairs={{128,0},{256,128},{384,256},{129,1},{257,129},{385,257},{130,2},{2... | collective-permute-start | bytes 245768 | tf_op jit(solution)/shard_map/ppermute | solution.py:20
  71.4 17.4 %collective-permute-start.6 = (bf16[128,320]{0,1:T(8,128)(2,1)}, bf16[128,320]{0,1:T(8,128)(2,1)}, u32[]{:S(2)}, u32[]{:S(2)}) collective-permute-start(bf16[128,320]{0,1:T(8,128)(2,1)} %collective-permute-done.5), channel_id=1, source_target_pairs={{0,256},{128,384},{256,0},{384,128},{1,257},{129,385},{257,1},{385... | collective-permute-start | bytes 245768 | tf_op jit(solution)/shard_map/ppermute | solution.py:14
  95.2 16.9 %collective-permute-start.8 = (bf16[128,320]{0,1:T(8,128)(2,1)S(1)}, bf16[128,320]{0,1:T(8,128)(2,1)}, u32[]{:S(2)}, u32[]{:S(2)}) collective-permute-start(bf16[128,320]{0,1:T(8,128)(2,1)S(1)} %get-tuple-element.599), channel_id=1, source_target_pairs={{0,128},{128,0},{256,384},{384,256},{1,129},{129,1},{257,385},{385... | collective-permute-start | bytes 245768 | tf_op jit(solution)/shard_map/ppermute | solution.py:14
  110.2 9.5 %collective-permute-start.10 = (bf16[128,320]{0,1:T(8,128)(2,1)}, bf16[128,320]{0,1:T(8,128)(2,1)}, u32[]{:S(2)}, u32[]{:S(2)}) collective-permute-start(bf16[128,320]{0,1:T(8,128)(2,1)} %get-tuple-element.600), channel_id=1, source_target_pairs={{128,0},{256,128},{384,256},{129,1},{257,129},{385,257},{130,2},{2... | collective-permute-start | bytes 245768 | tf_op jit(solution)/shard_map/ppermute | solution.py:20
  112.1 9.8 %collective-permute-start.9 = (bf16[128,320]{0,1:T(8,128)(2,1)}, bf16[128,320]{0,1:T(8,128)(2,1)}, u32[]{:S(2)}, u32[]{:S(2)}) collective-permute-start(bf16[128,320]{0,1:T(8,128)(2,1)} %collective-permute-done.8), channel_id=1, source_target_pairs={{0,256},{128,384},{256,0},{384,128},{1,257},{129,385},{257,1},{385... | collective-permute-start | bytes 245768 | tf_op jit(solution)/shard_map/ppermute | solution.py:14
  125.2 3.0 %copy-start.11 = (bf16[1280,320]{1,0:T(8,128)(2,1)S(1)}, bf16[1280,320]{1,0:T(8,128)(2,1)}, u32[]{:S(2)}) copy-start(bf16[1280,320]{1,0:T(8,128)(2,1)} %get-tuple-element.542) | copy-start | bytes 2457604 | tf_op jit(solution)/shard_map/cond
  128.6 2.9 %copy-start.18 = (bf16[2,128,320]{2,1,0:T(8,128)(2,1)S(1)}, bf16[2,128,320]{2,1,0:T(8,128)(2,1)}, u32[]{:S(2)}) copy-start(bf16[2,128,320]{2,1,0:T(8,128)(2,1)} %copy.62) | copy-start | bytes 491524 | tf_op jit(solution)/shard_map/cond
  135.0 3.2 %copy-start.22 = (bf16[128,320]{0,1:T(8,128)(2,1)S(1)}, bf16[128,320]{0,1:T(8,128)(2,1)}, u32[]{:S(2)}) copy-start(bf16[128,320]{0,1:T(8,128)(2,1)} %convolution_convert_fusion.3) | copy-start | bytes 245764 | tf_op jit(solution)/shard_map/cond
  138.2 6.9 %collective-permute-start.11 = (bf16[128,320]{0,1:T(8,128)(2,1)S(1)}, bf16[128,320]{0,1:T(8,128)(2,1)}, u32[]{:S(2)}, u32[]{:S(2)}) collective-permute-start(bf16[128,320]{0,1:T(8,128)(2,1)S(1)} %get-tuple-element.602), channel_id=1, source_target_pairs={{0,128},{128,0},{256,384},{384,256},{1,129},{129,1},{257,385},{385... | collective-permute-start | bytes 245768 | tf_op jit(solution)/shard_map/ppermute | solution.py:14
  143.2 7.2 %collective-permute-start.13 = (bf16[128,320]{0,1:T(8,128)(2,1)}, bf16[128,320]{0,1:T(8,128)(2,1)}, u32[]{:S(2)}, u32[]{:S(2)}) collective-permute-start(bf16[128,320]{0,1:T(8,128)(2,1)} %get-tuple-element.603), channel_id=1, source_target_pairs={{128,0},{256,128},{384,256},{129,1},{257,129},{385,257},{130,2},{2... | collective-permute-start | bytes 245768 | tf_op jit(solution)/shard_map/ppermute | solution.py:20
  145.1 10.4 %collective-permute-start.12 = (bf16[128,320]{0,1:T(8,128)(2,1)}, bf16[128,320]{0,1:T(8,128)(2,1)}, u32[]{:S(2)}, u32[]{:S(2)}) collective-permute-start(bf16[128,320]{0,1:T(8,128)(2,1)} %collective-permute-done.11), channel_id=1, source_target_pairs={{0,256},{128,384},{256,0},{384,128},{1,257},{129,385},{257,1},{385... | collective-permute-start | bytes 245768 | tf_op jit(solution)/shard_map/ppermute | solution.py:14
  159.1 4.2 %copy-start.12 = (bf16[1280,320]{1,0:T(8,128)(2,1)S(1)}, bf16[1280,320]{1,0:T(8,128)(2,1)}, u32[]{:S(2)}) copy-start(bf16[1280,320]{1,0:T(8,128)(2,1)} %get-tuple-element.637) | copy-start | bytes 2457604 | tf_op jit(solution)/shard_map/cond
  163.3 0.9 copy-start.2
  164.2 1.2 copy-start.15
  206.2 25.9 %all-to-all-start.1 = ((bf16[64,2,400]{2,1,0:T(2,128)(2,1)}), bf16[64,2,400]{2,1,0:T(2,128)(2,1)S(1)}, u32[]{:S(2)}, u32[]{:S(2)}) async-start(bf16[64,2,400]{2,1,0:T(2,128)(2,1)} %reshape.197), calls=%async_computation.1 | async-start | bytes 262144 | tf_op jit(solution)/shard_map/all_to_all | solution.py:38
  232.1 37.6 %all-to-all-start.3 = ((bf16[64,10,640]{2,1,0:T(8,128)(2,1)}), bf16[64,10,640]{2,1,0:T(8,128)(2,1)S(1)}, u32[]{:S(2)}, u32[]{:S(2)}) async-start(bf16[64,10,640]{2,1,0:T(8,128)(2,1)} %copy.68), calls=%async_computation.3 | async-start | bytes 2621440 | tf_op jit(solution)/shard_map/all_to_all | solution.py:38
  239.6 31.7 %copy-start.19 = (bf16[1,2,128,320]{2,3,1,0:T(8,128)(2,1)}, bf16[1,2,128,320]{2,3,1,0:T(8,128)(2,1)S(1)}, u32[]{:S(2)}) copy-start(bf16[1,2,128,320]{2,3,1,0:T(8,128)(2,1)S(1)} %bitcast_dynamic-update-slice_fusion) | copy-start | bytes 491524
where the time goes:
time: 274 us; the launch traced here: 271 us
  starting transfers between devices  108 us (39%)
  waiting for transfers between devices  55.7 us (20%)
  local copies, waits for them, and re-layouts  34.8 us (13%)
  other arithmetic  28.7 us (10%)
  matrix products  22.2 us (8%)
  blocking collectives  20.9 us (8%)
    ppermute x10, starting transfers between devices, from_partner(): lax.ppermute(shard, axis, [(i, i ^ 1 << stride) for i in range(lax.axis_s...  80.9 us
    all_to_all x2, waiting for transfers between devices, sum_by_axis(): lax.all_to_all(own.astype(jnp.bfloat16), far, 0, 0, tiled=True)  36.4 us
    all_to_all x2, starting transfers between devices, sum_by_axis(): lax.all_to_all(own.astype(jnp.bfloat16), far, 0, 0, tiled=True)  21.6 us
    all_to_all x2, blocking collectives, sum_at_owner(): lax.all_to_all(cut_along(shard, dim, length), axis, 0, 0, tiled=True)  20.9 us
    ppermute x10, waiting for transfers between devices, from_partner(): lax.ppermute(shard, axis, [(i, i ^ 1 << stride) for i in range(lax.axis_s...  19.3 us
    another operation x19, local copies, waits for them, and re-layouts  15.2 us
    dot_general x11, matrix products, contract(): lax.dot_general(left, right, ((dims[0], dims[1]), ((), ())), preferred_el...  14 us
    select_n x9, other arithmetic, put_micro(): return jnp.where(valid, updated, buffer)  8.34 us
  transfers between devices with their start and end apart: 16, of which 12 were waited for; matrix products, arithmetic and copies ran while one was open for 5% of the time, Pallas kernels for 0%

commit v1 on v0

v1 whole, which is shorter than its diff:
```python
import jax
import jax.numpy as jnp
from jax import lax
from jax.experimental import pallas as pl
from jax.experimental.pallas import tpu as pltpu
from jax.sharding import Mesh
from jax.sharding import PartitionSpec as P

DP = ("z", "x", "w", "core")
MESH = pl.DeviceIdType.MESH
EPS = 1e-06
CHUNKS = 4
F32 = jnp.float32
BF16 = jnp.bfloat16


def dot(left, right):
    return jnp.dot(left, right, preferred_element_type=F32)


def dot_nt(left, right):
    return lax.dot_general(left, right, (((1,), (1,)), ((), ())), preferred_element_type=F32)


def dot_tn(left, right):
    return lax.dot_general(left, right, (((0,), (0,)), ((), ())), preferred_element_type=F32)


def chain_kernel(
    x_ref,
    ts_ref,
    table_ref,
    wskip_ref,
    win_ref,
    wout_ref,
    cot_ref,
    grads_ref,
    din_ref,
    dout_ref,
    dskip_ref,
    z_buf,
    g_buf,
    k_buf,
    vsend,
    csend,
    ksend,
    u_buf,
    r_buf,
    n_buf,
    act_buf,
    ds_buf,
    gpre_buf,
    gyb_buf,
    vs_sem,
    vr_sem,
    cs_sem,
    cr_sem,
    ks_sem,
    kr_sem,
):
    section = lax.axis_index("section")
    rows = x_ref.shape[0] // CHUNKS
    micro, per = ts_ref.shape
    levels = table_ref.shape[0]

    barrier = pltpu.get_barrier_semaphore()
    for step in (1, 3):
        pl.semaphore_signal(
            barrier, inc=1, device_id={"section": lax.rem(section + step, 4)}, device_id_type=MESH
        )
    pl.semaphore_wait(barrier, 2)

    def at(c):
        return pl.ds(pl.multiple_of(c * rows, rows), rows)

    def value_copy(c):
        return pltpu.make_async_remote_copy(
            src_ref=vsend.at[at(c)],
            dst_ref=z_buf.at[at(c)],
            send_sem=vs_sem.at[c],
            recv_sem=vr_sem.at[c],
            device_id={"section": 3 - section},
            device_id_type=MESH,
        )

    def chain_copy(c):
        return pltpu.make_async_remote_copy(
            src_ref=csend.at[at(c)],
            dst_ref=g_buf.at[at(c)],
            send_sem=cs_sem.at[c],
            recv_sem=cr_sem.at[c],
            device_id={"section": lax.rem(section + 3, 4)},
            device_id_type=MESH,
        )

    def skip_copy(c):
        return pltpu.make_async_remote_copy(
            src_ref=ksend.at[at(c)],
            dst_ref=k_buf.at[at(c)],
            send_sem=ks_sem.at[c],
            recv_sem=kr_sem.at[c],
            device_id={"section": lax.rem(section + 1, 4)},
            device_id_type=MESH,
        )

    def forward(c, encoder):
        here = at(c)
        united = x_ref[here, :].astype(F32) + dot(z_buf[here, :], wskip_ref[...])
        recip = lax.rsqrt(jnp.mean(united * united, axis=-1, keepdims=True) + EPS)
        normed = (united * recip).astype(BF16)
        preact = dot_nt(normed, win_ref[...])
        sigma = jax.nn.sigmoid(preact)
        active = (preact * sigma).astype(BF16)
        u_buf[here, :] = united
        r_buf[here, :] = jnp.broadcast_to(recip, (rows, 128))
        n_buf[here, :] = normed
        act_buf[here, :] = active
        ds_buf[here, :] = sigma * (1.0 + preact * (1.0 - sigma))
        if encoder:
            vsend[here, :] = (united + dot(active, wout_ref[...])).astype(BF16)
            value_copy(c).start()

    def backward(c):
        here = at(c)
        gy = g_buf[here, :].astype(F32) + k_buf[here, :].astype(F32)
        low = gy.astype(BF16)
        gyb_buf[here, :] = low
        pre = (dot_nt(low, wout_ref[...]) * ds_buf[here, :]).astype(BF16)
        gpre_buf[here, :] = pre
        gn = dot(pre, win_ref[...])
        united = u_buf[here, :]
        recip = r_buf[here, 0:1]
        mean = jnp.mean(gn * united, axis=-1, keepdims=True)
        chain = (gy + recip * gn - united * (recip * recip * recip * mean)).astype(BF16)
        grads_ref[here, :] = chain

        @pl.when(section == 1)
        def _():
            csend[here, :] = chain

        @pl.when(section >= 2)
        def _():
            back = dot_nt(chain, wskip_ref[...]).astype(BF16)

            @pl.when(section == 2)
            def _():
                csend[here, :] = (chain.astype(F32) + back.astype(F32)).astype(BF16)

            @pl.when(section == 3)
            def _():
                csend[here, :] = chain
                ksend[here, :] = back
                skip_copy(c).start()

        @pl.when(section > 0)
        def _():
            chain_copy(c).start()

    @pl.when(section > 0)
    def _():
        k_buf[...] = jnp.zeros_like(k_buf)

    @pl.when(section < 2)
    def _():
        for m in range(micro):
            column = jnp.broadcast_to(ts_ref[m : m + 1, :].astype(F32), (per, per)).T
            onehot = column[:, 0:1] == lax.broadcasted_iota(jnp.int32, (per, levels), 1).astype(F32)
            z_buf[m * per : (m + 1) * per, :] = dot(
                jnp.where(onehot, 1.0, 0.0).astype(BF16), table_ref[...]
            ).astype(BF16)

        @pl.loop(0, CHUNKS)
        def _(c):
            forward(c, True)

    @pl.when(section == 3)
    def _():
        g_buf[...] = cot_ref[...]

    @pl.when(section >= 2)
    def _():
        @pl.loop(0, CHUNKS)
        def _(c):
            value_copy(c).wait_recv()
            forward(c, False)

            @pl.when(section == 3)
            def _():
                backward(c)

    @pl.when(section < 3)
    def _():
        @pl.loop(0, CHUNKS)
        def _(c):
            chain_copy(c).wait_recv()

            @pl.when(section == 0)
            def _():
                skip_copy(c).wait_recv()

            backward(c)

    dout_ref[...] = dot_tn(act_buf[...], gyb_buf[...]).astype(BF16)
    din_ref[...] = dot_tn(gpre_buf[...], n_buf[...]).astype(BF16)
    dskip_ref[...] = dot_tn(z_buf[...], grads_ref[...]).astype(BF16)

    for c in range(CHUNKS):

        @pl.when(section < 2)
        def _():
            value_copy(c).wait_send()

        @pl.when(section > 0)
        def _():
            chain_copy(c).wait_send()

        @pl.when(section == 3)
        def _():
            skip_copy(c).wait_send()


def cut_along(shard, dim, length):
    before, after = (shard.shape[:dim], shard.shape[dim + 1 :])
    return jnp.moveaxis(shard.reshape(*before, length, -1, *after), dim, 0)


def sum_at_owner(shard, axis, dim):
    length = lax.axis_size(axis)
    blocks = lax.all_to_all(cut_along(shard, dim, length), axis, 0, 0, tiled=True)
    return jnp.sum(blocks.astype(jnp.float32), axis=0)


def sum_by_axis(shard, axes, dim):
    far, near = axes
    own = sum_at_owner(cut_along(shard, dim, lax.axis_size(far)), near, dim + 1)
    return jnp.sum(
        lax.all_to_all(own.astype(jnp.bfloat16), far, 0, 0, tiled=True).astype(jnp.float32), axis=0
    )


def sent_together(arrays, axis, dim, along):
    ends, at = ([], 0)
    for a in arrays[:-1]:
        at += a.shape[along]
        ends.append(at)
    both = jnp.concatenate(arrays, axis=along)
    return tuple(jnp.split(sum_by_axis(both, axis, dim), ends, axis=along))


def shards(saved_inputs, timesteps, time_table, skip_weight, ff_in, ff_out, output_cotangent):
    n_micro, per, width = saved_inputs.shape[1:]
    hidden = ff_in.shape[1]
    total = n_micro * per
    low = pltpu.VMEM((total, width), BF16)
    grads, d_in, d_out, d_skip = pl.pallas_call(
        chain_kernel,
        out_shape=(
            jax.ShapeDtypeStruct((total, width), BF16),
            jax.ShapeDtypeStruct((hidden, width), BF16),
            jax.ShapeDtypeStruct((hidden, width), BF16),
            jax.ShapeDtypeStruct((width, width), BF16),
        ),
        in_specs=[pl.BlockSpec(memory_space=pltpu.VMEM)] * 7,
        out_specs=(pl.BlockSpec(memory_space=pltpu.VMEM),) * 4,
        scratch_shapes=[
            low,
            low,
            low,
            low,
            low,
            low,
            pltpu.VMEM((total, width), F32),
            pltpu.VMEM((total, 128), F32),
            low,
            pltpu.VMEM((total, hidden), BF16),
            pltpu.VMEM((total, hidden), F32),
            pltpu.VMEM((total, hidden), BF16),
            low,
        ]
        + [pltpu.SemaphoreType.DMA((CHUNKS,))] * 6,
        compiler_params=pltpu.CompilerParams(collective_id=0, has_side_effects=True),
    )(
        saved_inputs.reshape(total, width),
        timesteps,
        time_table,
        skip_weight[0],
        ff_in[0],
        ff_out[0],
        output_cotangent.reshape(total, width),
    )
    axes = (("z", "x", "w"), "core")
    grad_in, grad_out = sent_together((d_in, d_out), axes, 0, 1)
    grad_skip = sum_by_axis(d_skip.reshape(-1), axes, 0)
    return (grads.reshape(1, n_micro, per, width), grad_skip[None], grad_in[None], grad_out[None])


def solution(mesh):
    split = Mesh(
        mesh.devices.reshape(mesh.shape["section"], 8, 4, 2, 2), ("section", "z", "x", "w", "core")
    )
    return jax.shard_map(
        shards,
        mesh=split,
        in_specs=(
            P("section", None, DP, None),
            P(None, DP),
            P(),
            P("section", None, None),
            P("section", None, None),
            P("section", None, None),
            P(None, DP, None),
        ),
        out_specs=(
            P("section", None, DP, None),
            P("section", DP),
            P("section", DP, None),
            P("section", DP, None),
        ),
        check_vma=False,
    )
```

time: 274 us -> 138 us (0.50)
  starting transfers between devices: 108 us -> 28 us
  Pallas kernels: 0 us -> 46.9 us
  other arithmetic: 28.7 us -> 4.75 us
  matrix products: 22.2 us -> 0 us
  blocking collectives: 20.9 us -> 0 us
  waiting for transfers between devices: 55.7 us -> 37.8 us
  local copies, waits for them, and re-layouts: 34.8 us -> 18.7 us
    ppermute x14 -> x0, starting transfers between devices: 86.1 us -> none  [the longest x10 80.9 us: from_partner(): lax.ppermute(shard, axis, [(i, i ^ 1 << stride) for i in range(lax.axis_s...]
    pallas_call x0 -> x1, Pallas kernels: none -> 46.9 us  [shards(): pl.pallas_call(chain_kernel, out_shape=(jax.ShapeDtypeStruct((total, widt...]
    dot_general x21 -> x0, matrix products: 22.2 us -> none  [the longest x11 14 us: contract(): lax.dot_general(left, right, ((dims[0], dims[1]), ((), ())), preferred_el...]
    all_to_all x2 -> x0, blocking collectives: 20.9 us -> none  [sum_at_owner(): lax.all_to_all(cut_along(shard, dim, length), axis, 0, 0, tiled=True)]
    ppermute x14 -> x0, waiting for transfers between devices: 19.3 us -> none  [the longest x10 19.3 us: from_partner(): lax.ppermute(shard, axis, [(i, i ^ 1 << stride) for i in range(lax.axis_s...]
    convert_element_type x8 -> x0, other arithmetic: 15.3 us -> none  [the longest x4 6.29 us: shards(): upstream = chain.astype(jnp.float32) + jnp.where(section < 2, carried, 0.0)]
    another operation x19 -> x0, local copies, waits for them, and re-layouts: 15.2 us -> none
    select_n x12 -> x0, other arithmetic: 11.4 us -> none  [the longest x9 8.34 us: put_micro(): return jnp.where(valid, updated, buffer)]
  transfers between devices with their start and end apart: 16 -> 4, of which waited for: 12 -> 3; matrix products, arithmetic and copies ran while one was open for 5% -> 10% of each run, Pallas kernels for 0% -> 0%
where the time goes in v1:
time: 138 us; the launch traced here: 137 us
  Pallas kernels  46.9 us (34%)
  waiting for transfers between devices  37.8 us (27%)
  starting transfers between devices  28 us (20%)
  local copies, waits for them, and re-layouts  18.7 us (14%)
  other arithmetic  4.75 us (3%)
    pallas_call x1, Pallas kernels, shards(): pl.pallas_call(chain_kernel, out_shape=(jax.ShapeDtypeStruct((total, widt...  46.9 us
    all_to_all x2, waiting for transfers between devices, sum_by_axis(): lax.all_to_all(own.astype(jnp.bfloat16), far, 0, 0, tiled=True)  37.7 us
    all_to_all x2, starting transfers between devices, sum_by_axis(): lax.all_to_all(own.astype(jnp.bfloat16), far, 0, 0, tiled=True)  18.9 us
    all_to_all x2, starting transfers between devices, sum_at_owner(): lax.all_to_all(cut_along(shard, dim, length), axis, 0, 0, tiled=True)  9.11 us
    unnamed x20, local copies, waits for them, and re-layouts  8.35 us
    another operation x3, local copies, waits for them, and re-layouts, cut_along(): return jnp.moveaxis(shard.reshape(*before, length, -1, *after), dim, 0)  4.67 us
    concatenate x1, other arithmetic, sent_together(): both = jnp.concatenate(arrays, axis=along)  2.89 us
  transfers between devices with their start and end apart: 4, of which 3 were waited for; matrix products, arithmetic and copies ran while one was open for 10% of the time, Pallas kernels for 0%

profile of v1, /device:TPU:1, one launch (start us, length us, event | category | flops | bytes accessed | tf_op | source)
XLA Modules:
  0.0 136.9 jit_solution(1970235916105993692)
XLA Ops:
  0.6 0.0 copy-start.1
  0.6 0.0 copy-start.2
  0.7 2.3 %copy.50 = bf16[1,1280,320]{2,1,0:T(8,128)(2,1)} copy(bf16[1,1280,320]{1,2,0:T(8,128)(2,1)} %param.11) | data formatting | bytes 1638400 | tf_op args[4]
  3.0 0.0 copy-done.1
  3.0 0.0 copy-start.4
  3.0 0.0 copy-start.5
  3.0 1.3 copy.51
  4.3 0.0 copy-done.2
  4.3 1.2 copy.53.table_ref
  5.5 0.0 copy-done.4
  5.5 0.8 copy.49
  6.3 0.0 copy-done.5
  6.3 0.8 copy.52
  7.1 46.9 %shard_map.102 = (bf16[256,320]{1,0:T(8,128)(2,1)}, bf16[1280,320]{1,0:T(8,128)(2,1)}, bf16[1280,320]{1,0:T(8,128)(2,1)}, bf16[320,320]{1,0:T(8,128)(2,1)}) custom-call(bf16[256,320]{1,0:T(8,128)(2,1)} %bitcast.14, s32[2,128]{1,0:T(2,128)} %ts_ref.1, bf16[1000,320]{1,0:T(8,128)(2,1)} %copy.53.table_ref, bf16[320,320]{1,0:T(8,128)(2,1)} %bitcast.17, ...), custom_call_target="tpu_custom_call" | custom-call | tf_op jit(solution)/shard_map/pallas_call | solution.py:255
  54.0 0.0 copy-start
  54.0 1.5 %reshape_reshape_reshape.3 = bf16[64,2,800]{2,1,0:T(2,128)(2,1)S(1)} reshape(bf16[320,320]{1,0:T(8,128)(2,1)} %get-tuple-element.9) | data formatting | bytes 409600 | tf_op jit(solution)/shard_map/reshape;reshape;reshape | solution.py:224
  55.5 0.7 copy.60
  56.2 5.4 %all-to-all-start = ((bf16[2,64,800]{2,1,0:T(8,128)(2,1)}), bf16[2,64,800]{2,1,0:T(8,128)(2,1)S(1)}, u32[]{:S(2)}, u32[]{:S(2)}) async-start(bf16[2,64,800]{2,1,0:T(8,128)(2,1)} %bitcast.10), calls=%async_computation | async-start | bytes 458752 | tf_op jit(solution)/shard_map/all_to_all | solution.py:229
  61.7 0.0 copy-done
  61.7 2.9 %pad_maximum_fusion = bf16[1280,640]{1,0:T(8,128)(2,1)} fusion(bf16[1280,320]{1,0:T(8,128)(2,1)} %get-tuple-element.11, bf16[1280,320]{1,0:T(8,128)(2,1)S(1)} %copy-done), kind=kLoop, calls=%fused_computation.1 | loop fusion | flops 3276800 | bytes 3276800 | tf_op jit(solution)/shard_map/concatenate | solution.py:246
  64.6 2.5 %reshape_reshape.3 = bf16[64,2,10,640]{3,2,1,0:T(8,128)(2,1)S(1)} reshape(bf16[1280,640]{1,0:T(8,128)(2,1)} %pad_maximum_fusion) | data formatting | bytes 3276800 | tf_op jit(solution)/shard_map/reshape;reshape | solution.py:224
  67.0 1.7 %copy.56 = bf16[2,64,10,640]{3,1,2,0:T(8,128)(2,1)} copy(bf16[2,64,10,640]{3,2,0,1:T(8,128)(2,1)S(1)} %bitcast.11) | data formatting | bytes 3276800 | tf_op jit(solution)/shard_map/transpose | solution.py:224
  68.7 0.0 all-to-all-done
  68.7 3.7 %all-to-all-start.2 = ((bf16[2,64,10,640]{3,1,2,0:T(8,128)(2,1)}), bf16[2,64,10,640]{3,1,2,0:T(8,128)(2,1)S(1)}, u32[]{:S(2)}, u32[]{:S(2)}) async-start(bf16[2,64,10,640]{3,1,2,0:T(8,128)(2,1)} %copy.56), calls=%async_computation.2 | async-start | bytes 3276800 | tf_op jit(solution)/shard_map/all_to_all | solution.py:229
  72.5 0.5 broadcast
  73.0 0.7 reduce.3
  73.7 0.8 reshape.23
  74.5 0.1 all-to-all-done.2
  74.6 13.5 %all-to-all-start.1 = ((bf16[64,2,400]{2,1,0:T(2,128)(2,1)}), bf16[64,2,400]{2,1,0:T(2,128)(2,1)S(1)}, u32[]{:S(2)}, u32[]{:S(2)}) async-start(bf16[64,2,400]{2,1,0:T(2,128)(2,1)} %reshape.23), calls=%async_computation.1 | async-start | bytes 262144 | tf_op jit(solution)/shard_map/all_to_all | solution.py:237
  88.1 0.7 reduce_sum.44
  88.8 1.6 %copy.57 = bf16[64,10,640]{2,1,0:T(8,128)(2,1)} copy(bf16[64,10,640]{2,0,1:T(8,128)(2,1)S(1)} %reduce_sum.44) | data formatting | bytes 1638400 | tf_op jit(solution)/shard_map/reduce_sum | solution.py:230
  90.4 0.0 copy-start.3
  90.4 7.4 %all-to-all-done.1 = bf16[64,2,400]{2,1,0:T(2,128)(2,1)S(1)} async-done(((bf16[64,2,400]{2,1,0:T(2,128)(2,1)}), bf16[64,2,400]{2,1,0:T(2,128)(2,1)S(1)}, u32[]{:S(2)}, u32[]{:S(2)}) %all-to-all-start.1) | async-done | bytes 102432 | tf_op jit(solution)/shard_map/all_to_all | solution.py:237
  97.8 5.4 %all-to-all-start.3 = ((bf16[64,10,640]{2,1,0:T(8,128)(2,1)}), bf16[64,10,640]{2,1,0:T(8,128)(2,1)S(1)}, u32[]{:S(2)}, u32[]{:S(2)}) async-start(bf16[64,10,640]{2,1,0:T(8,128)(2,1)} %copy.57), calls=%async_computation.3 | async-start | bytes 2621440 | tf_op jit(solution)/shard_map/all_to_all | solution.py:237
  103.2 0.0 copy-done.3
  103.2 0.8 copy.58
  104.0 0.2 reshape.24
  104.2 0.2 convert_reduce_fusion.1
  104.5 0.6 broadcast_in_dim.9
  105.0 30.3 %all-to-all-done.3 = bf16[64,10,640]{2,1,0:T(8,128)(2,1)S(1)} async-done(((bf16[64,10,640]{2,1,0:T(8,128)(2,1)}), bf16[64,10,640]{2,1,0:T(8,128)(2,1)S(1)}, u32[]{:S(2)}, u32[]{:S(2)}) %all-to-all-start.3) | async-done | bytes 819232 | tf_op jit(solution)/shard_map/all_to_all | solution.py:237
  135.4 0.2 convert_reduce_fusion
  135.6 0.1 fusion
  135.7 0.6 broadcast_in_dim.10
  136.3 0.6 broadcast_in_dim.11
  (1 shorter events, 0.0 us)
Async XLA Ops:
  0.6 2.4 %copy-start.1 = (bf16[1,1280,320]{1,2,0:T(8,128)(2,1)S(1)}, bf16[1,1280,320]{1,2,0:T(8,128)(2,1)}, u32[]{:S(2)}) copy-start(bf16[1,1280,320]{1,2,0:T(8,128)(2,1)} %param.12) | copy-start | bytes 2457604
  0.6 3.7 %copy-start.2 = (bf16[1000,320]{0,1:T(8,128)(2,1)S(1)}, bf16[1000,320]{0,1:T(8,128)(2,1)}, u32[]{:S(2)}) copy-start(bf16[1000,320]{0,1:T(8,128)(2,1)} %param.9) | copy-start | bytes 1920004
  3.0 2.5 %copy-start.4 = (bf16[1,2,128,320]{2,3,1,0:T(8,128)(2,1)S(1)}, bf16[1,2,128,320]{2,3,1,0:T(8,128)(2,1)}, u32[]{:S(2)}) copy-start(bf16[1,2,128,320]{2,3,1,0:T(8,128)(2,1)} %param.7) | copy-start | bytes 491524
  3.0 3.3 %copy-start.5 = (bf16[2,128,320]{1,2,0:T(8,128)(2,1)S(1)}, bf16[2,128,320]{1,2,0:T(8,128)(2,1)}, u32[]{:S(2)}) copy-start(bf16[2,128,320]{1,2,0:T(8,128)(2,1)} %param.13) | copy-start | bytes 491524
  54.0 7.6 %copy-start = (bf16[1280,320]{1,0:T(8,128)(2,1)S(1)}, bf16[1280,320]{1,0:T(8,128)(2,1)}, u32[]{:S(2)}) copy-start(bf16[1280,320]{1,0:T(8,128)(2,1)} %get-tuple-element.10) | copy-start | bytes 2457604
  56.2 12.5 %all-to-all-start = ((bf16[2,64,800]{2,1,0:T(8,128)(2,1)}), bf16[2,64,800]{2,1,0:T(8,128)(2,1)S(1)}, u32[]{:S(2)}, u32[]{:S(2)}) async-start(bf16[2,64,800]{2,1,0:T(8,128)(2,1)} %bitcast.10), calls=%async_computation | async-start | bytes 458752 | tf_op jit(solution)/shard_map/all_to_all | solution.py:229
  68.7 5.9 %all-to-all-start.2 = ((bf16[2,64,10,640]{3,1,2,0:T(8,128)(2,1)}), bf16[2,64,10,640]{3,1,2,0:T(8,128)(2,1)S(1)}, u32[]{:S(2)}, u32[]{:S(2)}) async-start(bf16[2,64,10,640]{3,1,2,0:T(8,128)(2,1)} %copy.56), calls=%async_computation.2 | async-start | bytes 3276800 | tf_op jit(solution)/shard_map/all_to_all | solution.py:229
  74.6 23.2 %all-to-all-start.1 = ((bf16[64,2,400]{2,1,0:T(2,128)(2,1)}), bf16[64,2,400]{2,1,0:T(2,128)(2,1)S(1)}, u32[]{:S(2)}, u32[]{:S(2)}) async-start(bf16[64,2,400]{2,1,0:T(2,128)(2,1)} %reshape.23), calls=%async_computation.1 | async-start | bytes 262144 | tf_op jit(solution)/shard_map/all_to_all | solution.py:237
  90.4 12.8 %copy-start.3 = (bf16[256,320]{1,0:T(8,128)(2,1)S(1)}, bf16[256,320]{1,0:T(8,128)(2,1)}, u32[]{:S(2)}) copy-start(bf16[256,320]{1,0:T(8,128)(2,1)} %get-tuple-element.8) | copy-start | bytes 491524
  97.8 37.6 %all-to-all-start.3 = ((bf16[64,10,640]{2,1,0:T(8,128)(2,1)}), bf16[64,10,640]{2,1,0:T(8,128)(2,1)S(1)}, u32[]{:S(2)}, u32[]{:S(2)}) async-start(bf16[64,10,640]{2,1,0:T(8,128)(2,1)} %copy.57), calls=%async_computation.3 | async-start | bytes 2621440 | tf_op jit(solution)/shard_map/all_to_all | solution.py:237
